TPU v7x, 32 devices: a whole 2x2x4 slice. The times are simulated.
32 devices in a mesh: prompt: 8 (over z, core), ctx: 4 (over y, x).
Axes of the slice: x: 2, y: 2, z: 4, core: 2. Of those that a mesh axis runs over, the one named last changes fastest.
Arguments:
- queries: bfloat16 [16384, 16, 128], P(('prompt', 'ctx')), may hold values from -8 to 8
- keys: bfloat16 [16384, 4, 128], P(('prompt', 'ctx')), may hold values from -8 to 8
- values: bfloat16 [16384, 4, 128], P(('prompt', 'ctx')), may hold values from -6 to 6
- spans: int32 [8, 2], P('prompt'), may hold values from 1 to 1536, as said below
- partner: int32 [8], replicated, may hold values from 0 to 7, each once
Outputs:
- attended: bfloat16 [16384, 16, 128], P(('prompt', 'ctx'))
- decode_cache: bfloat16 [8, 2, 8, 4, 256, 128], P('ctx', None, 'prompt')
Inputs may be any that keep to these rules, and one draw needn't show every extreme that they name: `spans`: column 0 counts the image tokens of a prompt, from 512 to 1024, which come first; column 1 counts the text tokens after them, 1 or more; the two sum to at most 2048, and to exactly 2048 for at least one prompt.
All inputs are finite; a program needn't handle non-finite values.
Results may differ from a plain program's by a relative error of at most 0.0041.
Values may be sent and summed in bfloat16 or wider, within the bound.
A program may use at most 64 MiB of HBM per device.

v0:
```python
import math

import jax
import jax.numpy as jnp
from jax import lax
from jax.sharding import PartitionSpec as P

far_below = -1e30


def start_state(query):
    lead_shape = query.shape[:3]
    return (
        jnp.full(lead_shape, far_below, jnp.float32),
        jnp.zeros(lead_shape, jnp.float32),
        jnp.zeros(query.shape, jnp.float32),
    )


def key_block(progress, query, query_pos, block_keys, block_values, key_first, length):
    running_peak, row_total, accumulated = progress
    score_scale = 1.0 / math.sqrt(query.shape[-1])
    scores = (
        jnp.einsum("qgmd,kgd->qgmk", query, block_keys, preferred_element_type=jnp.float32)
        * score_scale
    )
    key_pos = key_first + lax.iota(jnp.int32, block_keys.shape[0])
    allowed = ((key_pos[None, :] <= query_pos[:, None]) & (key_pos[None, :] < length))[
        :, None, None, :
    ]
    scores = jnp.where(allowed, scores, far_below)
    new_peak = jnp.maximum(running_peak, jnp.max(scores, axis=-1))
    weights = jnp.where(allowed, jnp.exp(scores - new_peak[..., None]), 0.0)
    factor = jnp.exp(running_peak - new_peak)
    row_total = row_total * factor + jnp.sum(weights, axis=-1)
    accumulated = accumulated * factor[..., None] + jnp.einsum(
        "qgmk,kgd->qgmd",
        weights.astype(jnp.bfloat16),
        block_values,
        preferred_element_type=jnp.float32,
    )
    return (new_peak, row_total, accumulated)


def fold_keys(progress, query, query_pos, query_last, all_keys, all_values, length, limit):
    key_step = math.gcd(all_keys.shape[0], limit)
    block_count = all_keys.shape[0] // key_step
    key_blocks = all_keys.reshape(block_count, key_step, all_keys.shape[1], all_keys.shape[2])
    value_blocks = all_values.reshape(
        block_count, key_step, all_values.shape[1], all_values.shape[2]
    )

    def visit_block(carried, block_item):
        block_keys, block_values, block_index = block_item
        key_first = block_index * key_step
        needed = (key_first < length) & (key_first <= query_last)
        carried = lax.cond(
            needed,
            lambda held: key_block(
                held, query, query_pos, block_keys, block_values, key_first, length
            ),
            lambda held: held,
            carried,
        )
        return (carried, None)

    progress, ignored = lax.scan(
        visit_block, progress, (key_blocks, value_blocks, jnp.arange(block_count, dtype=jnp.int32))
    )
    return progress


def finish(progress, query_pos, length):
    running_peak, row_total, accumulated = progress
    mixture = accumulated / row_total[..., None]
    mixture = jnp.where((query_pos < length)[:, None, None, None], mixture, 0.0)
    return mixture.reshape(
        mixture.shape[0], mixture.shape[1] * mixture.shape[2], mixture.shape[3]
    ).astype(jnp.bfloat16)


def per_device(queries, keys, values, spans, partner):
    tok_rows, head_count, head_width = queries.shape
    kv_heads = keys.shape[1]
    members = head_count // kv_heads
    ctx_index = lax.axis_index("ctx")
    length = spans[0, 0] + spans[0, 1]
    stripes = lax.axis_size("prompt") // kv_heads
    live_rows = (ctx_index * tok_rows + lax.iota(jnp.int32, tok_rows) < length)[:, None, None]
    handoff = jnp.stack(
        [
            jnp.where(live_rows, keys, jnp.zeros_like(keys)),
            jnp.where(live_rows, values, jnp.zeros_like(values)),
        ]
    )
    handoff = handoff.reshape(1, 2, tok_rows // stripes, stripes * kv_heads, head_width)
    handoff = lax.all_to_all(handoff, "prompt", split_axis=3, concat_axis=0, tiled=True)
    handoff = jnp.take(handoff, partner, axis=0)
    handoff = handoff.reshape(handoff.shape[0], 2, 1, 1, tok_rows // stripes, head_width)
    handoff = lax.all_to_all(handoff, "ctx", split_axis=0, concat_axis=3, tiled=True)
    grouped = queries.reshape(tok_rows, kv_heads, members, head_width)
    query_pos = ctx_index * tok_rows + lax.iota(jnp.int32, tok_rows)
    query_last = ctx_index * tok_rows + tok_rows - 1
    progress = fold_keys(
        start_state(grouped),
        grouped,
        query_pos,
        query_last,
        lax.all_gather(keys, "ctx", axis=0, tiled=True),
        lax.all_gather(values, "ctx", axis=0, tiled=True),
        length,
        512,
    )
    attended = finish(progress, query_pos, length)
    return (attended, handoff)


def solution(mesh):
    placed = (
        P(("prompt", "ctx"), None, None),
        P(("prompt", "ctx"), None, None),
        P(("prompt", "ctx"), None, None),
        P("prompt", None),
        P(),
    )
    return jax.shard_map(
        per_device,
        mesh=mesh,
        in_specs=placed,
        out_specs=(P(("prompt", "ctx"), None, None), P("ctx", None, "prompt", None, None, None)),
        check_vma=False,
    )
```

profile of v0, /device:TPU:6, one launch (start us, length us, event | category | flops | bytes accessed | tf_op | source)
XLA Modules:
  0.0 182.5 jit_solution(7011516643668339774)
XLA Ops:
  7.2 0.0 all-gather.3.cloned.1.call-start
  7.2 1.9 %copy.29 = bf16[512,4,128]{2,0,1:T(8,128)(2,1)} copy(bf16[512,4,128]{2,1,0:T(4,128)(2,1)} %param.10) | data formatting | bytes 1048576 | tf_op args[1]
  9.1 0.0 all-gather.3.cloned.1.call-update
  9.1 0.0 all-gather.5.cloned.1.call-start
  9.2 1.9 %copy.31 = bf16[512,4,128]{2,0,1:T(8,128)(2,1)} copy(bf16[512,4,128]{2,1,0:T(4,128)(2,1)} %param.11) | data formatting | bytes 1048576 | tf_op args[2]
  11.1 1.3 fusion.21
  13.8 3.2 %broadcast_select_fusion.1 = (bf16[512,4,128]{2,1,0:T(4,128)(2,1)S(1)}, bf16[512,4,128]{2,1,0:T(4,128)(2,1)S(1)}) fusion(bf16[512,4,128]{2,1,0:T(4,128)(2,1)} %param.10, pred[512]{0:T(512)(128)(4,1)S(1)} %add_compare_fusion, bf16[512,4,128]{2,1,0:T(4,128)(2,1)} %param.11), kind=kLoop, calls=%fused_computation.31 | loop fusion | flops 524288 | bytes 2097664 | tf_op jit(solution)/shard_map/jit(_where)/select_n | solution.py:92
  17.0 0.1 pad_maximum_fusion
  17.1 1.2 copy.35
  18.3 4.9 %all-to-all-start = ((bf16[1,2,256,8,128]{4,2,1,0,3:T(8,128)(2,1)}), bf16[1,2,256,8,128]{4,2,1,0,3:T(8,128)(2,1)S(1)}, u32[]{:S(2)}, u32[]{:S(2)}) async-start(bf16[1,2,256,8,128]{4,2,1,0,3:T(8,128)(2,1)} %copy.35), calls=%async_computation | async-start | bytes 2097152 | tf_op jit(solution)/shard_map/all_to_all | solution.py:97
  23.2 26.5 %all-to-all-done = bf16[1,2,256,8,128]{4,2,1,0,3:T(8,128)(2,1)S(1)} async-done(((bf16[1,2,256,8,128]{4,2,1,0,3:T(8,128)(2,1)}), bf16[1,2,256,8,128]{4,2,1,0,3:T(8,128)(2,1)S(1)}, u32[]{:S(2)}, u32[]{:S(2)}) %all-to-all-start) | async-done | bytes 1048608 | tf_op jit(solution)/shard_map/all_to_all | solution.py:97
  49.7 0.7 gather_fusion
  50.5 1.1 fusion.20
  51.6 4.2 %all-to-all-start.1 = ((bf16[8,2,1,1,256,128]{5,4,1,3,2,0:T(8,128)(2,1)}), bf16[8,2,1,1,256,128]{5,4,1,3,2,0:T(8,128)(2,1)S(1)}, u32[]{:S(2)}, u32[]{:S(2)}) async-start(bf16[8,2,1,1,256,128]{5,4,1,3,2,0:T(8,128)(2,1)} %fusion.20), calls=%async_computation.1 | async-start | bytes 2097152 | tf_op jit(solution)/shard_map/all_to_all | solution.py:100
  55.8 2.3 %copy.30 = bf16[512,16,128]{2,0,1:T(8,128)(2,1)S(1)} copy(bf16[512,16,128]{2,1,0:T(8,128)(2,1)} %param.9) | data formatting | bytes 4194304 | tf_op args[0]
  58.0 15.1 %all-to-all-done.1 = bf16[8,2,1,1,256,128]{5,4,1,3,2,0:T(8,128)(2,1)S(1)} async-done(((bf16[8,2,1,1,256,128]{5,4,1,3,2,0:T(8,128)(2,1)}), bf16[8,2,1,1,256,128]{5,4,1,3,2,0:T(8,128)(2,1)S(1)}, u32[]{:S(2)}, u32[]{:S(2)}) %all-to-all-start.1) | async-done | bytes 1048608 | tf_op jit(solution)/shard_map/all_to_all | solution.py:100
  73.2 1.0 copy.37
  74.2 3.1 %copy.32 = bf16[4,512,4,128]{3,1,2,0:T(8,128)(2,1)} copy(bf16[4,512,4,128]{3,1,0,2:T(8,128)(2,1)} %bitcast.68) | data formatting | bytes 4194304
  77.3 13.6 %all-gather.5.cloned.1.call-done = bf16[2048,4,128]{2,0,1:T(8,128)(2,1)} async-done(((bf16[512,4,128]{2,0,1:T(8,128)(2,1)}), bf16[2048,4,128]{2,0,1:T(8,128)(2,1)}) %all-gather.5.cloned.1.call-update) | async-done | bytes 2097168 | tf_op jit(solution)/shard_map/all_gather | solution.py:110
  90.9 3.1 %copy.33 = bf16[4,512,4,128]{3,1,2,0:T(8,128)(2,1)} copy(bf16[4,512,4,128]{3,1,0,2:T(8,128)(2,1)} %bitcast.69) | data formatting | bytes 4194304
  94.0 2.4 %broadcast_in_dim.79 = f32[512,4,4,128]{3,0,2,1:T(8,128)} broadcast(f32[]{:T(128)} %constant.62.clone.1), dimensions={} | broadcast | bytes 4194308 | tf_op jit(solution)/shard_map/broadcast_in_dim | solution.py:16
  96.4 72.6 %while.15 = (s32[]{:T(128)}, f32[512,4,4]{0,2,1:T(4,128)S(1)}, f32[512,4,4]{0,2,1:T(4,128)S(1)}, f32[512,4,4,128]{3,0,2,1:T(8,128)}, s32[4]{0:T(128)S(1)}, /*ind...) while((s32[]{:T(128)}, f32[512,4,4]{0,2,1:T(4,128)S(1)}, ...), condition=%wide.region_5.6_spmd.clone, body=%wide.region_0.5_spmd.clone.sunk | while | flops 2204649472 | bytes 63453520 | solution.py:67
  96.4 0.6 dynamic_slice.33
  97.7 16.9 %conditional.3 = ((f32[512,4,4]{0,2,1:T(4,128)S(1)}, f32[512,4,4]{0,2,1:T(4,128)S(1)}, f32[512,4,4,128]{3,0,2,1:T(8,128)})) conditional(s32[]{:T(128)} %convert_element_type.23, (f32[512,4,4]{0,2,1:T(4,128)S(1)}, f32[512,4,4]{0,2,1:T(4,128)S(1)}, f32[512,4,4,128]{3,0,2,1:T(8,128)}) %tuple.52, (s32[]{:T(128)}, s32[]{:T(128)}, s32[]{:T(128)}, ...), branch_computations={%region_1.1_spmd, %region_2.4_spmd} | conditional | flops 2204649472 | bytes 63451184 | solution.py:57
  97.7 0.2 compare_and_fusion
  98.0 3.8 %fusion.2 = (f32[512,4,4]{0,2,1:T(4,128)S(1)}, f32[4,512,512,4]{2,1,3,0:T(8,128)S(1)}) fusion(pred[512,512]{0,1:T(8,128)(4,1)S(1)} %compare_and_fusion, bf16[512,4,4,128]{3,0,2,1:T(8,128)(2,1)S(1)} %get-tuple-element.127, bf16[4,512,4,128]{3,1,2,0:T(8,128)(2,1)} %get-tuple-element.125, s32[]{:T(128)} %get-tuple-element.126), kind=kOutput, calls=%fused_computation.4 | convolution fusion | flops 1086316544 | bytes 19694080 | tf_op jit(solution)/shard_map/while/body/eval_jaxpr/cond/branch_1_fun/qgmd,kgd->qgmk/dot_general | solution.py:24
  101.8 4.0 %fusion.4 = f32[512,4,4]{0,2,1:T(4,128)S(1)} fusion(f32[4,512,512,4]{2,1,3,0:T(8,128)S(1)} %get-tuple-element.247, f32[512,4,4]{0,2,1:T(4,128)S(1)} %max.4, pred[512,512]{0,1:T(8,128)(4,1)S(1)} %compare_and_fusion), kind=kLoop, calls=%fused_computation.6 | loop fusion | flops 20963328 | bytes 17104896 | tf_op jit(solution)/shard_map/while/body/eval_jaxpr/cond/branch_1_fun/reduce_sum | solution.py:35
  105.9 8.7 %bitcast_add_fusion = f32[512,4,4,128]{3,0,2,1:T(8,128)} fusion(f32[512,4,4,128]{3,0,2,1:T(8,128)} %get-tuple-element.129, f32[4,512,512,4]{2,1,3,0:T(8,128)S(1)} %get-tuple-element.247, f32[512,4,4]{0,2,1:T(4,128)S(1)} %max.4, pred[512,512]{0,1:T(8,128)(4,1)S(1)} %compare_and_fusion, f32[512,4,4]{0,2,1:T(4,128)S(1)} %bitcast.75, ...), kind=kOutput, calls=%fused_computation.9 | convolution fusion | flops 1096810496 | bytes 26018304 | tf_op jit(solution)/shard_map/while/body/eval_jaxpr/cond/branch_1_fun/qgmk,kgd->qgmd/dot_general | solution.py:36
  114.6 0.6 dynamic_slice.33
  115.8 16.9 %conditional.3 = ((f32[512,4,4]{0,2,1:T(4,128)S(1)}, f32[512,4,4]{0,2,1:T(4,128)S(1)}, f32[512,4,4,128]{3,0,2,1:T(8,128)})) conditional(s32[]{:T(128)} %convert_element_type.23, (f32[512,4,4]{0,2,1:T(4,128)S(1)}, f32[512,4,4]{0,2,1:T(4,128)S(1)}, f32[512,4,4,128]{3,0,2,1:T(8,128)}) %tuple.52, (s32[]{:T(128)}, s32[]{:T(128)}, s32[]{:T(128)}, ...), branch_computations={%region_1.1_spmd, %region_2.4_spmd} | conditional | flops 2204649472 | bytes 63451184 | solution.py:57
  115.9 0.2 compare_and_fusion
  116.1 3.8 %fusion.2 = (f32[512,4,4]{0,2,1:T(4,128)S(1)}, f32[4,512,512,4]{2,1,3,0:T(8,128)S(1)}) fusion(pred[512,512]{0,1:T(8,128)(4,1)S(1)} %compare_and_fusion, bf16[512,4,4,128]{3,0,2,1:T(8,128)(2,1)S(1)} %get-tuple-element.127, bf16[4,512,4,128]{3,1,2,0:T(8,128)(2,1)} %get-tuple-element.125, s32[]{:T(128)} %get-tuple-element.126), kind=kOutput, calls=%fused_computation.4 | convolution fusion | flops 1086316544 | bytes 19694080 | tf_op jit(solution)/shard_map/while/body/eval_jaxpr/cond/branch_1_fun/qgmd,kgd->qgmk/dot_general | solution.py:24
  120.0 4.0 %fusion.4 = f32[512,4,4]{0,2,1:T(4,128)S(1)} fusion(f32[4,512,512,4]{2,1,3,0:T(8,128)S(1)} %get-tuple-element.247, f32[512,4,4]{0,2,1:T(4,128)S(1)} %max.4, pred[512,512]{0,1:T(8,128)(4,1)S(1)} %compare_and_fusion), kind=kLoop, calls=%fused_computation.6 | loop fusion | flops 20963328 | bytes 17104896 | tf_op jit(solution)/shard_map/while/body/eval_jaxpr/cond/branch_1_fun/reduce_sum | solution.py:35
  124.0 8.7 %bitcast_add_fusion = f32[512,4,4,128]{3,0,2,1:T(8,128)} fusion(f32[512,4,4,128]{3,0,2,1:T(8,128)} %get-tuple-element.129, f32[4,512,512,4]{2,1,3,0:T(8,128)S(1)} %get-tuple-element.247, f32[512,4,4]{0,2,1:T(4,128)S(1)} %max.4, pred[512,512]{0,1:T(8,128)(4,1)S(1)} %compare_and_fusion, f32[512,4,4]{0,2,1:T(4,128)S(1)} %bitcast.75, ...), kind=kOutput, calls=%fused_computation.9 | convolution fusion | flops 1096810496 | bytes 26018304 | tf_op jit(solution)/shard_map/while/body/eval_jaxpr/cond/branch_1_fun/qgmk,kgd->qgmd/dot_general | solution.py:36
  132.7 0.6 dynamic_slice.33
  134.0 16.9 %conditional.3 = ((f32[512,4,4]{0,2,1:T(4,128)S(1)}, f32[512,4,4]{0,2,1:T(4,128)S(1)}, f32[512,4,4,128]{3,0,2,1:T(8,128)})) conditional(s32[]{:T(128)} %convert_element_type.23, (f32[512,4,4]{0,2,1:T(4,128)S(1)}, f32[512,4,4]{0,2,1:T(4,128)S(1)}, f32[512,4,4,128]{3,0,2,1:T(8,128)}) %tuple.52, (s32[]{:T(128)}, s32[]{:T(128)}, s32[]{:T(128)}, ...), branch_computations={%region_1.1_spmd, %region_2.4_spmd} | conditional | flops 2204649472 | bytes 63451184 | solution.py:57
  134.0 0.2 compare_and_fusion
  134.3 3.8 %fusion.2 = (f32[512,4,4]{0,2,1:T(4,128)S(1)}, f32[4,512,512,4]{2,1,3,0:T(8,128)S(1)}) fusion(pred[512,512]{0,1:T(8,128)(4,1)S(1)} %compare_and_fusion, bf16[512,4,4,128]{3,0,2,1:T(8,128)(2,1)S(1)} %get-tuple-element.127, bf16[4,512,4,128]{3,1,2,0:T(8,128)(2,1)} %get-tuple-element.125, s32[]{:T(128)} %get-tuple-element.126), kind=kOutput, calls=%fused_computation.4 | convolution fusion | flops 1086316544 | bytes 19694080 | tf_op jit(solution)/shard_map/while/body/eval_jaxpr/cond/branch_1_fun/qgmd,kgd->qgmk/dot_general | solution.py:24
  138.1 4.0 %fusion.4 = f32[512,4,4]{0,2,1:T(4,128)S(1)} fusion(f32[4,512,512,4]{2,1,3,0:T(8,128)S(1)} %get-tuple-element.247, f32[512,4,4]{0,2,1:T(4,128)S(1)} %max.4, pred[512,512]{0,1:T(8,128)(4,1)S(1)} %compare_and_fusion), kind=kLoop, calls=%fused_computation.6 | loop fusion | flops 20963328 | bytes 17104896 | tf_op jit(solution)/shard_map/while/body/eval_jaxpr/cond/branch_1_fun/reduce_sum | solution.py:35
  142.2 8.7 %bitcast_add_fusion = f32[512,4,4,128]{3,0,2,1:T(8,128)} fusion(f32[512,4,4,128]{3,0,2,1:T(8,128)} %get-tuple-element.129, f32[4,512,512,4]{2,1,3,0:T(8,128)S(1)} %get-tuple-element.247, f32[512,4,4]{0,2,1:T(4,128)S(1)} %max.4, pred[512,512]{0,1:T(8,128)(4,1)S(1)} %compare_and_fusion, f32[512,4,4]{0,2,1:T(4,128)S(1)} %bitcast.75, ...), kind=kOutput, calls=%fused_computation.9 | convolution fusion | flops 1096810496 | bytes 26018304 | tf_op jit(solution)/shard_map/while/body/eval_jaxpr/cond/branch_1_fun/qgmk,kgd->qgmd/dot_general | solution.py:36
  150.9 0.6 dynamic_slice.33
  152.1 16.9 %conditional.3 = ((f32[512,4,4]{0,2,1:T(4,128)S(1)}, f32[512,4,4]{0,2,1:T(4,128)S(1)}, f32[512,4,4,128]{3,0,2,1:T(8,128)})) conditional(s32[]{:T(128)} %convert_element_type.23, (f32[512,4,4]{0,2,1:T(4,128)S(1)}, f32[512,4,4]{0,2,1:T(4,128)S(1)}, f32[512,4,4,128]{3,0,2,1:T(8,128)}) %tuple.52, (s32[]{:T(128)}, s32[]{:T(128)}, s32[]{:T(128)}, ...), branch_computations={%region_1.1_spmd, %region_2.4_spmd} | conditional | flops 2204649472 | bytes 63451184 | solution.py:57
  152.2 0.2 compare_and_fusion
  152.4 3.8 %fusion.2 = (f32[512,4,4]{0,2,1:T(4,128)S(1)}, f32[4,512,512,4]{2,1,3,0:T(8,128)S(1)}) fusion(pred[512,512]{0,1:T(8,128)(4,1)S(1)} %compare_and_fusion, bf16[512,4,4,128]{3,0,2,1:T(8,128)(2,1)S(1)} %get-tuple-element.127, bf16[4,512,4,128]{3,1,2,0:T(8,128)(2,1)} %get-tuple-element.125, s32[]{:T(128)} %get-tuple-element.126), kind=kOutput, calls=%fused_computation.4 | convolution fusion | flops 1086316544 | bytes 19694080 | tf_op jit(solution)/shard_map/while/body/eval_jaxpr/cond/branch_1_fun/qgmd,kgd->qgmk/dot_general | solution.py:24
  156.3 4.0 %fusion.4 = f32[512,4,4]{0,2,1:T(4,128)S(1)} fusion(f32[4,512,512,4]{2,1,3,0:T(8,128)S(1)} %get-tuple-element.247, f32[512,4,4]{0,2,1:T(4,128)S(1)} %max.4, pred[512,512]{0,1:T(8,128)(4,1)S(1)} %compare_and_fusion), kind=kLoop, calls=%fused_computation.6 | loop fusion | flops 20963328 | bytes 17104896 | tf_op jit(solution)/shard_map/while/body/eval_jaxpr/cond/branch_1_fun/reduce_sum | solution.py:35
  160.3 8.7 %bitcast_add_fusion = f32[512,4,4,128]{3,0,2,1:T(8,128)} fusion(f32[512,4,4,128]{3,0,2,1:T(8,128)} %get-tuple-element.129, f32[4,512,512,4]{2,1,3,0:T(8,128)S(1)} %get-tuple-element.247, f32[512,4,4]{0,2,1:T(4,128)S(1)} %max.4, pred[512,512]{0,1:T(8,128)(4,1)S(1)} %compare_and_fusion, f32[512,4,4]{0,2,1:T(4,128)S(1)} %bitcast.75, ...), kind=kOutput, calls=%fused_computation.9 | convolution fusion | flops 1096810496 | bytes 26018304 | tf_op jit(solution)/shard_map/while/body/eval_jaxpr/cond/branch_1_fun/qgmk,kgd->qgmd/dot_general | solution.py:36
  169.0 3.7 %select_convert_fusion = bf16[512,4,4,128]{3,0,2,1:T(8,128)(2,1)S(1)} fusion(f32[512,4,4,128]{3,0,2,1:T(8,128)} %get-tuple-element.150, f32[512,4,4]{0,2,1:T(4,128)S(1)} %get-tuple-element.151, pred[512]{0:T(512)(128)(4,1)S(1)} %add_compare_fusion), kind=kLoop, calls=%fused_computation.26 | loop fusion | flops 3145728 | bytes 6324736 | tf_op jit(solution)/shard_map/convert_element_type | solution.py:79
  172.7 2.9 %copy.34 = bf16[512,4,4,128]{3,2,1,0:T(4,128)(2,1)} copy(bf16[512,4,4,128]{3,0,2,1:T(8,128)(2,1)S(1)} %select_convert_fusion) | data formatting | bytes 4194304 | tf_op jit(solution)/shard_map/convert_element_type | solution.py:79
  (35 shorter events, 0.3 us)
Async XLA Ops:
  7.2 67.0 %all-gather.3.cloned.1.call-start = ((), (), s32[]{:S(2)}) async-start(), calls=%async_computation.2 | async-start | bytes 2621440 | tf_op jit(solution)/shard_map/all_gather | solution.py:109
  9.1 81.7 %all-gather.5.cloned.1.call-start = ((), (), s32[]{:S(2)}) async-start(), calls=%async_computation.3 | async-start | bytes 2621440 | tf_op jit(solution)/shard_map/all_gather | solution.py:110
  13.7 9.4 %copy-start = (s32[8]{0:T(128)S(1)}, s32[8]{0:T(128)}, u32[]{:S(2)}) copy-start(s32[8]{0:T(128)} %param.13) | copy-start | bytes 100
  18.3 31.4 %all-to-all-start = ((bf16[1,2,256,8,128]{4,2,1,0,3:T(8,128)(2,1)}), bf16[1,2,256,8,128]{4,2,1,0,3:T(8,128)(2,1)S(1)}, u32[]{:S(2)}, u32[]{:S(2)}) async-start(bf16[1,2,256,8,128]{4,2,1,0,3:T(8,128)(2,1)} %copy.35), calls=%async_computation | async-start | bytes 2097152 | tf_op jit(solution)/shard_map/all_to_all | solution.py:97
  51.6 21.6 %all-to-all-start.1 = ((bf16[8,2,1,1,256,128]{5,4,1,3,2,0:T(8,128)(2,1)}), bf16[8,2,1,1,256,128]{5,4,1,3,2,0:T(8,128)(2,1)S(1)}, u32[]{:S(2)}, u32[]{:S(2)}) async-start(bf16[8,2,1,1,256,128]{5,4,1,3,2,0:T(8,128)(2,1)} %fusion.20), calls=%async_computation.1 | async-start | bytes 2097152 | tf_op jit(solution)/shard_map/all_to_all | solution.py:100
Sparse Core Ops, SparseCore 0:
  10.4 35.4 all-gather.2
  47.7 43.1 all-gather.4
where the time goes:
time: 184 us; the launch traced here: 183 us
  waiting for transfers between devices  55.2 us (30%)
  matrix products  50 us (27%)
  other arithmetic  25.4 us (14%)
  local copies, waits for them, and re-layouts  24.4 us (13%)
  between operations  15.4 us (8%)
  starting transfers between devices  9.15 us (5%)
  loops' own time  2.89 us (2%)
    dot_general x4, matrix products, key_block(): jnp.einsum('qgmk,kgd->qgmd', weights.astype(jnp.bfloat16), block_values,...  34.7 us
    all_to_all x1, waiting for transfers between devices, per_device(): lax.all_to_all(handoff, 'prompt', split_axis=3, concat_axis=0, tiled=True)  26.5 us
    reduce_sum x4, other arithmetic, key_block(): row_total = row_total * factor + jnp.sum(weights, axis=-1)  16.1 us
    dot_general x4, matrix products, key_block(): jnp.einsum('qgmd,kgd->qgmk', query, block_keys, preferred_element_type=jn...  15.3 us
    all_to_all x1, waiting for transfers between devices, per_device(): lax.all_to_all(handoff, 'ctx', split_axis=0, concat_axis=3, tiled=True)  15.1 us
    all_gather x1, waiting for transfers between devices, per_device(): lax.all_gather(values, 'ctx', axis=0, tiled=True)  13.6 us
    unnamed x8, local copies, waits for them, and re-layouts  13.4 us
    all_to_all x1, starting transfers between devices, per_device(): lax.all_to_all(handoff, 'prompt', split_axis=3, concat_axis=0, tiled=True)  4.88 us
  transfers between devices with their start and end apart: 4, of which 3 were waited for; matrix products, arithmetic and copies ran while one was open for 9% of the time, Pallas kernels for 0%

commit v1 on v0

v1 whole, which is shorter than its diff:
```python
import functools
import math

import jax
import jax.numpy as jnp
from jax import lax
from jax.experimental import pallas as pl
from jax.experimental.pallas import tpu as pltpu
from jax.sharding import PartitionSpec as P

far_below = -1e30
MESH = pl.DeviceIdType.MESH
f32, bf16 = jnp.float32, jnp.bfloat16


def prep_kernel(spans_ref, base_ref, k_ref, v_ref, out_ref, tmp):
    groups, _, stripes, rows, _ = out_ref.shape
    length = spans_ref[0, 0] + spans_ref[0, 1]
    row = lax.broadcasted_iota(jnp.int32, (rows, 1), 0)
    for t, ref in enumerate((k_ref, v_ref)):
        tmp[t] = ref[...].astype(f32)
        for st in range(stripes):
            live = base_ref[0] + row * stripes + st < length
            for g in range(groups):
                x = tmp[t, pl.ds(st * groups + g, rows, stride=stripes * groups), :]
                out_ref[g, t, st] = jnp.where(live, x, 0.0).astype(bf16)


def main_kernel(
    n_prompt,
    n_ctx,
    spans_ref,
    partner_ref,
    q_ref,
    kv_ref,
    att_ref,
    dec_ref,
    kvbuf,
    hand1,
    hand2,
    tmp,
    qh,
    acc,
    peak,
    bias,
    own_sem,
    kv_send,
    kv_recv,
    h1_send,
    h1_recv,
    h2_send,
    h2_recv,
):
    tok, heads, width = q_ref.shape
    groups, _, stripes, rows, _ = kv_ref.shape
    members = heads // groups
    per_ctx = dec_ref.shape[0]
    me_p = lax.axis_index("prompt")
    me = lax.axis_index("ctx")
    length = spans_ref[0, 0] + spans_ref[0, 1]
    scale = math.log2(math.e) / math.sqrt(width)

    own = pltpu.make_async_copy(kv_ref, kvbuf.at[me], own_sem)
    own.start()

    barrier = pltpu.get_barrier_semaphore()
    for k in range(1, n_prompt):
        pl.semaphore_signal(
            barrier, inc=1, device_id={"prompt": lax.rem(me_p + k, n_prompt)}, device_id_type=MESH
        )
    for k in range(1, n_ctx):
        pl.semaphore_signal(
            barrier, inc=1, device_id={"ctx": lax.rem(me + k, n_ctx)}, device_id_type=MESH
        )
    own.wait()
    pl.semaphore_wait(barrier, n_prompt + n_ctx - 2)

    def kv_copy(dest, block, g):
        return pltpu.make_async_remote_copy(
            src_ref=kvbuf.at[block, g],
            dst_ref=kvbuf.at[block, g],
            send_sem=kv_send.at[dest, g],
            recv_sem=kv_recv.at[block, g],
            device_id={"ctx": dest},
            device_id_type=MESH,
        )

    def h1_copy(slot):
        return pltpu.make_async_remote_copy(
            src_ref=kvbuf.at[me, lax.rem(slot, groups), :, lax.div(slot, groups)],
            dst_ref=hand1.at[me_p],
            send_sem=h1_send.at[slot],
            recv_sem=h1_recv.at[me_p],
            device_id={"prompt": slot},
            device_id_type=MESH,
        )

    def h2_copy(dest):
        return pltpu.make_async_remote_copy(
            src_ref=hand2.at[pl.ds(dest * per_ctx, per_ctx)],
            dst_ref=dec_ref.at[:, :, 0, me],
            send_sem=h2_send.at[dest],
            recv_sem=h2_recv.at[me],
            device_id={"ctx": dest},
            device_id_type=MESH,
        )

    own1 = pltpu.make_async_copy(
        kvbuf.at[me, lax.rem(me_p, groups), :, lax.div(me_p, groups)],
        hand1.at[me_p],
        h1_send.at[me_p],
    )
    own2 = pltpu.make_async_copy(
        hand2.at[pl.ds(me * per_ctx, per_ctx)], dec_ref.at[:, :, 0, me], h2_send.at[me]
    )

    def send_group(g, carry):
        def send_one(k, carry):
            kv_copy(n_ctx - k, me, g).start()
            return carry

        lax.fori_loop(1, n_ctx - me, send_one, 0)
        return carry

    lax.fori_loop(0, groups, send_group, 0)
    own1.start()
    for k in range(1, n_prompt):
        h1_copy(lax.rem(me_p + k, n_prompt)).start()

    tmp[...] = q_ref[...].reshape(tok * heads, width).astype(f32)
    for h in range(heads):
        qh[h] = tmp[pl.ds(h, tok, stride=heads), :].astype(bf16)
    col = lax.broadcasted_iota(jnp.int32, (1, tok), 1)
    key_pos = lax.rem(col, rows) * stripes + lax.div(col, rows)
    row_pos = lax.broadcasted_iota(jnp.int32, (tok, 1), 0)
    bias[...] = jnp.where(
        (key_pos <= row_pos) & (key_pos + me * tok < length), 0.0, far_below
    )
    ones = jnp.ones((tok, width), bf16)
    tile = tok // 2

    def attend(block, g, first):
        keys = kvbuf[block, g, 0].reshape(tok, width)
        mixed = jnp.concatenate([kvbuf[block, g, 1].reshape(tok, width), ones], axis=1)
        if not first:
            row_bias = jnp.where(key_pos + block * tok < length, 0.0, far_below)

        def one_head(m, carry):
            h = g * members + m
            for start in range(0, tok, tile):
                part = pl.ds(start, tile)
                scores = lax.dot_general(
                    qh[h, part, :], keys, (((1,), (1,)), ((), ())), preferred_element_type=f32
                )
                scores = scores * scale + (bias[part, :] if first else row_bias)
                top = jnp.max(scores, axis=1, keepdims=True)
                if not first:
                    before = peak[h, part, :]
                    top = jnp.maximum(top, before)
                weights = jnp.exp2(scores - top).astype(bf16)
                mixture = jnp.dot(weights, mixed, preferred_element_type=f32)
                if not first:
                    mixture = mixture + acc[h, part, :] * jnp.exp2(before - top)
                acc[h, part, :] = mixture
                peak[h, part, :] = top
            return carry

        lax.fori_loop(0, members, one_head, 0)

    def diagonal(g, carry):
        attend(me, g, True)
        return carry

    lax.fori_loop(0, groups, diagonal, 0)

    def stage_two():
        own1.wait()
        for k in range(1, n_prompt):
            h1_copy(lax.rem(me_p + k, n_prompt)).wait_send()
        for k in range(1, n_prompt):
            source = lax.rem(me_p + k, n_prompt)
            pltpu.make_async_copy(hand1.at[source], hand1.at[source], h1_recv.at[source]).wait()
        for b in range(n_prompt):
            hand2[b] = hand1[partner_ref[b]]

    def stage_two_send():
        own2.start()
        for k in range(1, n_ctx):
            h2_copy(lax.rem(me + k, n_ctx)).start()

    def earlier(step, carry):
        @pl.when(step <= me)
        def _():
            def one(g, carry):
                kv_copy(me, me - step, g).wait_recv()
                attend(me - step, g, False)
                return carry

            lax.fori_loop(0, groups, one, 0)

        @pl.when(step == 1)
        def _():
            stage_two()
            stage_two_send()

        return carry

    lax.fori_loop(1, n_ctx, earlier, 0)

    query_live = row_pos + me * tok < length
    for h in range(heads):
        result = acc[h, :, :width] / acc[h, :, width:]
        tmp[pl.ds(h, tok, stride=heads), :] = jnp.where(query_live, result, 0.0)
    att_ref[...] = tmp[...].astype(bf16).reshape(tok, heads, width)

    def drain_group(g, carry):
        def drain_one(k, carry):
            kv_copy(n_ctx - k, me, g).wait_send()
            return carry

        lax.fori_loop(1, n_ctx - me, drain_one, 0)
        return carry

    lax.fori_loop(0, groups, drain_group, 0)
    own2.wait()
    for k in range(1, n_ctx):
        h2_copy(lax.rem(me + k, n_ctx)).wait_send()
    for k in range(1, n_ctx):
        source = lax.rem(me + k, n_ctx)
        landed = dec_ref.at[:, :, 0, source]
        pltpu.make_async_copy(landed, landed, h2_recv.at[source]).wait()


def per_device(n_prompt, n_ctx, queries, keys, values, spans, partner):
    tok, heads, width = queries.shape
    groups = keys.shape[1]
    stripes = n_prompt // groups
    rows = tok // stripes
    per_ctx = partner.shape[0] // n_ctx
    vmem = pl.BlockSpec(memory_space=pltpu.VMEM)
    smem = pl.BlockSpec(memory_space=pltpu.SMEM)
    base = (lax.axis_index("ctx") * tok).astype(jnp.int32).reshape(1)
    kv = pl.pallas_call(
        prep_kernel,
        out_shape=jax.ShapeDtypeStruct((groups, 2, stripes, rows, width), bf16),
        in_specs=[smem, smem, vmem, vmem],
        out_specs=vmem,
        scratch_shapes=[pltpu.VMEM((2, tok * groups, width), f32)],
        name="prep",
    )(spans, base, keys.reshape(tok * groups, width), values.reshape(tok * groups, width))
    dma = pltpu.SemaphoreType.DMA
    attended, cache = pl.pallas_call(
        functools.partial(main_kernel, n_prompt, n_ctx),
        out_shape=(
            jax.ShapeDtypeStruct((tok, heads, width), bf16),
            jax.ShapeDtypeStruct((per_ctx, 2, 1, n_ctx, rows, width), bf16),
        ),
        in_specs=[smem, smem, vmem, pl.BlockSpec(memory_space=pl.ANY)],
        out_specs=(vmem, vmem),
        scratch_shapes=[
            pltpu.VMEM((n_ctx, groups, 2, stripes, rows, width), bf16),
            pltpu.VMEM((n_prompt, 2, rows, width), bf16),
            pltpu.VMEM((n_prompt, 2, rows, width), bf16),
            pltpu.VMEM((tok * heads, width), f32),
            pltpu.VMEM((heads, tok, width), bf16),
            pltpu.VMEM((heads, tok, 2 * width), f32),
            pltpu.VMEM((heads, tok, 1), f32),
            pltpu.VMEM((tok, tok), f32),
            dma,
            dma((n_ctx, groups)),
            dma((n_ctx, groups)),
            dma((n_prompt,)),
            dma((n_prompt,)),
            dma((n_ctx,)),
            dma((n_ctx,)),
        ],
        compiler_params=pltpu.CompilerParams(
            collective_id=0, has_side_effects=True, vmem_limit_bytes=60 * 1024 * 1024
        ),
        name="attend",
    )(spans, partner, queries, kv)
    return (attended, cache)


def solution(mesh):
    placed = (
        P(("prompt", "ctx"), None, None),
        P(("prompt", "ctx"), None, None),
        P(("prompt", "ctx"), None, None),
        P("prompt", None),
        P(),
    )
    return jax.shard_map(
        functools.partial(per_device, mesh.shape["prompt"], mesh.shape["ctx"]),
        mesh=mesh,
        in_specs=placed,
        out_specs=(P(("prompt", "ctx"), None, None), P("ctx", None, "prompt", None, None, None)),
        check_vma=False,
    )
```

time: 184 us -> 83.6 us (0.45)
  Pallas kernels: 0 us -> 78.2 us
  waiting for transfers between devices: 55.2 us -> 0 us
  matrix products: 50 us -> 0 us
  other arithmetic: 25.4 us -> 0 us
  local copies, waits for them, and re-layouts: 24.4 us -> 4.33 us
  between operations: 15.4 us -> 0.65 us
  starting transfers between devices: 9.15 us -> 0 us
  loops' own time: 2.89 us -> 0 us
    pallas_call x0 -> x2, Pallas kernels: none -> 78.2 us  [the longest x1 75.3 us: per_device(): pl.pallas_call(functools.partial(main_kernel, n_prompt, n_ctx), out_shape...]
    dot_general x8 -> x0, matrix products: 50 us -> none  [the longest x4 34.7 us: key_block(): jnp.einsum('qgmk,kgd->qgmd', weights.astype(jnp.bfloat16), block_values,...]
    all_to_all x2 -> x0, waiting for transfers between devices: 41.6 us -> none  [the longest x1 26.5 us: per_device(): lax.all_to_all(handoff, 'prompt', split_axis=3, concat_axis=0, tiled=True)]
    reduce_sum x4 -> x0, other arithmetic: 16.1 us -> none  [key_block(): row_total = row_total * factor + jnp.sum(weights, axis=-1)]
    all_gather x2 -> x0, waiting for transfers between devices: 13.6 us -> none  [the longest x1 13.6 us: per_device(): lax.all_gather(values, 'ctx', axis=0, tiled=True)]
    all_to_all x2 -> x0, starting transfers between devices: 9.07 us -> none  [the longest x1 4.88 us: per_device(): lax.all_to_all(handoff, 'prompt', split_axis=3, concat_axis=0, tiled=True)]
    unnamed x8 -> x4, local copies, waits for them, and re-layouts: 13.4 us -> 4.33 us
    select_n x3 -> x0, other arithmetic: 4.34 us -> none  [the longest x1 3.2 us: per_device(): jnp.where(live_rows, keys, jnp.zeros_like(keys))]
  transfers between devices with their start and end apart: 4 -> 0, of which waited for: 3 -> 0; matrix products, arithmetic and copies ran while one was open for 9% -> 0% of each run, Pallas kernels for 0% -> 0%
where the time goes in v1:
time: 83.6 us; the launch traced here: 83.2 us
  Pallas kernels  78.2 us (94%)
  local copies, waits for them, and re-layouts  4.33 us (5%)
    pallas_call x1, Pallas kernels, per_device(): pl.pallas_call(functools.partial(main_kernel, n_prompt, n_ctx), out_shape...  75.3 us
    unnamed x4, local copies, waits for them, and re-layouts  4.33 us
    pallas_call x1, Pallas kernels, per_device(): pl.pallas_call(prep_kernel, out_shape=jax.ShapeDtypeStruct((groups, 2, st...  2.89 us

profile of v1, /device:TPU:6, one launch (start us, length us, event | category | flops | bytes accessed | tf_op | source)
XLA Modules:
  0.0 83.2 jit_solution(9842711093200548295)
XLA Ops:
  0.6 2.9 %prep.1.kv_ref = bf16[4,2,2,256,128]{4,3,2,1,0:T(8,128)(2,1)} custom-call(s32[1,2]{1,0:T(1,128)} %spans_ref.3, s32[1]{0:T(128)} %bitcast.base_ref, bf16[2048,128]{1,0:T(8,128)(2,1)} %bitcast.3, bf16[2048,128]{1,0:T(8,128)(2,1)} %bitcast.4), custom_call_target="tpu_custom_call" | custom-call | tf_op jit(solution)/shard_map/prep/pallas_call | solution.py:243
  3.5 75.3 %attend.1 = (bf16[512,16,128]{2,1,0:T(8,128)(2,1)}, bf16[2,2,1,4,256,128]{5,4,3,2,1,0:T(8,128)(2,1)}) custom-call(s32[1,2]{1,0:T(1,128)} %spans_ref.3, s32[8]{0:T(128)} %partner_ref.1, bf16[512,16,128]{2,1,0:T(8,128)(2,1)} %q_ref.1, bf16[4,2,2,256,128]{4,3,2,1,0:T(8,128)(2,1)} %prep.1.kv_ref), custom_call_target="tpu_custom_call" | custom-call | tf_op jit(solution)/shard_map/attend/pallas_call | solution.py:252
  78.8 0.0 copy-start
  78.8 3.4 %copy.9 = bf16[512,16,128]{2,1,0:T(8,128)(2,1)} copy(bf16[512,16,128]{2,1,0:T(8,128)(2,1)} %get-tuple-element.4) | data formatting | bytes 4194304
  82.2 0.0 copy-done
  82.2 1.0 %copy.10 = bf16[2,2,1,4,256,128]{5,4,3,2,1,0:T(8,128)(2,1)} copy(bf16[2,2,1,4,256,128]{5,4,3,2,1,0:T(8,128)(2,1)S(1)} %copy-done) | data formatting | bytes 2097152
Async XLA Ops:
  78.8 3.4 %copy-start = (bf16[2,2,1,4,256,128]{5,4,3,2,1,0:T(8,128)(2,1)S(1)}, bf16[2,2,1,4,256,128]{5,4,3,2,1,0:T(8,128)(2,1)}, u32[]{:S(2)}) copy-start(bf16[2,2,1,4,256,128]{5,4,3,2,1,0:T(8,128)(2,1)} %get-tuple-element.5) | copy-start | bytes 3145732

commit v2 on v1

--- a/solution.py
+++ b/solution.py
@@ -50,6 +50,7 @@
     h1_recv,
     h2_send,
     h2_recv,
+    relay_send,
 ):
     tok, heads, width = q_ref.shape
     groups, _, stripes, rows, _ = kv_ref.shape
@@ -114,15 +115,37 @@
         hand2.at[pl.ds(me * per_ctx, per_ctx)], dec_ref.at[:, :, 0, me], h2_send.at[me]
     )
 
-    def send_group(g, carry):
-        def send_one(k, carry):
-            kv_copy(n_ctx - k, me, g).start()
+    square = n_ctx == 4
+    half = groups // 2
+
+    def relay_copy(dest, block, g):
+        return pltpu.make_async_remote_copy(
+            src_ref=kvbuf.at[block, g],
+            dst_ref=kvbuf.at[block, g],
+            send_sem=relay_send.at[g],
+            recv_sem=kv_recv.at[block, g],
+            device_id={"ctx": dest},
+            device_id_type=MESH,
+        )
+
+    def each_send(act):
+        def one_group(g, carry):
+            for dest in range(n_ctx - 1, 0, -1):
+                wanted = me < dest
+                if square and dest == 3:
+                    wanted = (me == 1) | (me == 2)
+                if square and dest == 2:
+                    wanted = me == 0
+
+                @pl.when(wanted)
+                def _():
+                    act(kv_copy(dest, me, g))
+
             return carry
 
-        lax.fori_loop(1, n_ctx - me, send_one, 0)
-        return carry
-
-    lax.fori_loop(0, groups, send_group, 0)
+        lax.fori_loop(0, groups, one_group, 0)
+
+    each_send(lambda copy: copy.start())
     own1.start()
     for k in range(1, n_prompt):
         h1_copy(lax.rem(me_p + k, n_prompt)).start()
@@ -145,7 +168,7 @@
         if not first:
             row_bias = jnp.where(key_pos + block * tok < length, 0.0, far_below)
 
-        def one_head(m, carry):
+        def one_head(m):
             h = g * members + m
             for start in range(0, tok, tile):
                 part = pl.ds(start, tile)
@@ -163,9 +186,9 @@
                     mixture = mixture + acc[h, part, :] * jnp.exp2(before - top)
                 acc[h, part, :] = mixture
                 peak[h, part, :] = top
-            return carry
-
-        lax.fori_loop(0, members, one_head, 0)
+
+        for m in range(members):
+            one_head(m)
 
     def diagonal(g, carry):
         attend(me, g, True)
@@ -191,9 +214,32 @@
     def earlier(step, carry):
         @pl.when(step <= me)
         def _():
+            block = me - step
+            if square:
+                block = jnp.where(me == 2, step - 1, block)
+
             def one(g, carry):
-                kv_copy(me, me - step, g).wait_recv()
-                attend(me - step, g, False)
+                if square:
+                    @pl.when(jnp.logical_not((me == 3) & (step == 2)))
+                    def _():
+                        kv_copy(me, block, g).wait_recv()
+
+                    @pl.when((me == 1) & (g < half))
+                    def _():
+                        relay_copy(3, 0, g).start()
+
+                    @pl.when((me == 2) & (step == 1) & (g >= half))
+                    def _():
+                        relay_copy(3, 0, g).start()
+                else:
+                    kv_copy(me, block, g).wait_recv()
+                attend(block, g, False)
+                if square:
+                    @pl.when((me == 3) & (step == 1))
+                    def _():
+                        kv_copy(me, 1, g).wait_recv()
+                        relay_copy(2, 1, g).start()
+
                 return carry
 
             lax.fori_loop(0, groups, one, 0)
@@ -206,6 +252,16 @@
         return carry
 
     lax.fori_loop(1, n_ctx, earlier, 0)
+
+    def each_relay(act):
+        for g in range(groups):
+            @pl.when((me == 1) if g < half else (me == 2))
+            def _():
+                act(relay_copy(3, 0, g))
+
+            @pl.when(me == 3)
+            def _():
+                act(relay_copy(2, 1, g))
 
     query_live = row_pos + me * tok < length
     for h in range(heads):
@@ -213,15 +269,9 @@
         tmp[pl.ds(h, tok, stride=heads), :] = jnp.where(query_live, result, 0.0)
     att_ref[...] = tmp[...].astype(bf16).reshape(tok, heads, width)
 
-    def drain_group(g, carry):
-        def drain_one(k, carry):
-            kv_copy(n_ctx - k, me, g).wait_send()
-            return carry
-
-        lax.fori_loop(1, n_ctx - me, drain_one, 0)
-        return carry
-
-    lax.fori_loop(0, groups, drain_group, 0)
+    each_send(lambda copy: copy.wait_send())
+    if square:
+        each_relay(lambda copy: copy.wait_send())
     own2.wait()
     for k in range(1, n_ctx):
         h2_copy(lax.rem(me + k, n_ctx)).wait_send()
@@ -273,6 +323,7 @@
             dma((n_prompt,)),
             dma((n_ctx,)),
             dma((n_ctx,)),
+            dma((groups,)),
         ],
         compiler_params=pltpu.CompilerParams(
             collective_id=0, has_side_effects=True, vmem_limit_bytes=60 * 1024 * 1024

time: 83.6 us -> 67 us (0.80)
  Pallas kernels: 78.2 us -> 61.8 us
    pallas_call x1, Pallas kernels: 75.3 us -> 58.9 us  [per_device(): pl.pallas_call(functools.partial(main_kernel, n_prompt, n_ctx), out_shape...]
where the time goes in v2:
time: 67 us; the launch traced here: 66.8 us
  Pallas kernels  61.8 us (92%)
  local copies, waits for them, and re-layouts  4.33 us (6%)
    pallas_call x1, Pallas kernels, per_device(): pl.pallas_call(functools.partial(main_kernel, n_prompt, n_ctx), out_shape...  58.9 us
    unnamed x4, local copies, waits for them, and re-layouts  4.33 us
    pallas_call x1, Pallas kernels, per_device(): pl.pallas_call(prep_kernel, out_shape=jax.ShapeDtypeStruct((groups, 2, st...  2.89 us

profile of v2, /device:TPU:6, one launch (start us, length us, event | category | flops | bytes accessed | tf_op | source)
XLA Modules:
  0.0 66.8 jit_solution(6274304029578152580)
XLA Ops:
  0.6 2.9 %prep.1.kv_ref = bf16[4,2,2,256,128]{4,3,2,1,0:T(8,128)(2,1)} custom-call(s32[1,2]{1,0:T(1,128)} %spans_ref.3, s32[1]{0:T(128)} %bitcast.base_ref, bf16[2048,128]{1,0:T(8,128)(2,1)} %bitcast.3, bf16[2048,128]{1,0:T(8,128)(2,1)} %bitcast.4), custom_call_target="tpu_custom_call" | custom-call | tf_op jit(solution)/shard_map/prep/pallas_call | solution.py:293
  3.5 58.9 %attend.1 = (bf16[512,16,128]{2,1,0:T(8,128)(2,1)}, bf16[2,2,1,4,256,128]{5,4,3,2,1,0:T(8,128)(2,1)}) custom-call(s32[1,2]{1,0:T(1,128)} %spans_ref.3, s32[8]{0:T(128)} %partner_ref.1, bf16[512,16,128]{2,1,0:T(8,128)(2,1)} %q_ref.1, bf16[4,2,2,256,128]{4,3,2,1,0:T(8,128)(2,1)} %prep.1.kv_ref), custom_call_target="tpu_custom_call" | custom-call | tf_op jit(solution)/shard_map/attend/pallas_call | solution.py:302
  62.4 0.0 copy-start
  62.4 3.4 %copy.9 = bf16[512,16,128]{2,1,0:T(8,128)(2,1)} copy(bf16[512,16,128]{2,1,0:T(8,128)(2,1)} %get-tuple-element.4) | data formatting | bytes 4194304
  65.8 0.0 copy-done
  65.8 1.0 %copy.10 = bf16[2,2,1,4,256,128]{5,4,3,2,1,0:T(8,128)(2,1)} copy(bf16[2,2,1,4,256,128]{5,4,3,2,1,0:T(8,128)(2,1)S(1)} %copy-done) | data formatting | bytes 2097152
Async XLA Ops:
  62.4 3.4 %copy-start = (bf16[2,2,1,4,256,128]{5,4,3,2,1,0:T(8,128)(2,1)S(1)}, bf16[2,2,1,4,256,128]{5,4,3,2,1,0:T(8,128)(2,1)}, u32[]{:S(2)}) copy-start(bf16[2,2,1,4,256,128]{5,4,3,2,1,0:T(8,128)(2,1)} %get-tuple-element.5) | copy-start | bytes 3145732
